TPU v7x, 32 devices: a 4x4x1 block of a 4x4x8 slice. The times are simulated.
32 devices in a mesh: dp: 1 (over z), tp: 32 (over y, x, core).
Axes of the slice: x: 4, y: 4, z: 1, core: 2. Of those that a mesh axis runs over, the one named last changes fastest.
The devices are a block of a 4x4x8 slice.
Arguments:
- X: bfloat16 [256, 4096], P('dp')
- W: bfloat16 [4096, 32768], P(None, 'tp')
- labels: int32 [256], P('dp')
Outputs:
- output 1: float32 [1], P('dp')
- output 2: bfloat16 [4096, 32768], P('dp', 'tp')
- output 3: bfloat16 [256, 4096], P('dp')
All inputs are finite; a program needn't handle non-finite values.
Results may differ from a plain program's by a relative error of at most 0.001.
Values are sent between devices in bfloat16 or wider.
A program may use at most 768 MiB of HBM per device.

v0:
```python
import jax
import jax.numpy as jnp
from jax import lax
from jax.sharding import PartitionSpec as P


def solution(mesh):
    def local(X, W, labels):
        T = X.shape[0]
        Vl = W.shape[1]
        off = lax.axis_index('tp') * Vl
        Z = jnp.dot(X, W, preferred_element_type=jnp.float32)
        m = Z.max(axis=1)
        s = jnp.exp(Z - m[:, None]).sum(axis=1)
        hit = jnp.arange(Vl, dtype=jnp.int32)[None, :] == (labels - off)[:, None]
        z = jnp.where(hit, Z, 0.0).sum(axis=1)
        M = lax.pmax(m, 'tp')
        st = lax.psum(jnp.stack([s * jnp.exp(m - M), z]), 'tp')
        S, zt = st[0], st[1]
        L = jnp.mean(M + jnp.log(S) - zt).reshape(1)
        G = ((jnp.exp(Z - M[:, None]) / S[:, None] - hit.astype(jnp.float32)) / T).astype(jnp.bfloat16)
        dW = jnp.einsum('th,tv->hv', X, G, preferred_element_type=jnp.float32).astype(jnp.bfloat16)
        dXp = jnp.einsum('tv,hv->th', G, W, preferred_element_type=jnp.float32)
        dX = lax.psum(dXp, 'tp').astype(jnp.bfloat16)
        return L, dW, dX

    return jax.shard_map(local, mesh=mesh,
                         in_specs=(P('dp', None), P(None, 'tp'), P('dp')),
                         out_specs=(P('dp'), P('dp', 'tp'), P('dp', None)),
                         check_vma=False)
```

profile of v0, /device:TPU:97, one launch (start us, length us, event | category | flops | bytes accessed | tf_op | source)
XLA Modules:
  0.0 208.0 jit_solution(15401219260200085344)
XLA Ops:
  0.6 0.0 copy-start
  0.6 1.6 copy-done
  2.2 0.0 copy-start.1
  2.2 5.8 %fusion.2 = (f32[256]{0:T(256)S(1)}, f32[256,1024]{1,0:T(8,128)S(1)}) fusion(bf16[256,4096]{1,0:T(8,128)(2,1)S(1)} %copy-done, bf16[4096,1024]{1,0:T(8,128)(2,1)} %param.4), kind=kOutput, calls=%fused_computation.11 | convolution fusion | flops 2147745536 | bytes 11535360 | tf_op jit(solution)/shard_map/dot_general | solution.py:12
  8.0 0.0 copy-done.1
  8.1 0.4 exponential_reduce_fusion
  8.4 49.8 %pmax.7 = f32[256]{0:T(256)S(1)} all-reduce(f32[256]{0:T(256)S(1)} %get-tuple-element.10), channel_id=1, replica_groups=mesh['dp'=1,'tp'=32] {'tp'}, use_global_device_ids=true, to_apply=%region_1.0 | all-reduce | flops 256 | bytes 2048 | tf_op jit(solution)/shard_map/pmax | solution.py:17
  58.3 43.5 %psum.14 = f32[2,256]{1,0:T(2,128)S(1)} all-reduce(f32[2,256]{1,0:T(2,128)S(1)} %pad_maximum_fusion), channel_id=1, replica_groups=mesh['dp'=1,'tp'=32] {'tp'}, use_global_device_ids=true, to_apply=%region_4.5 | all-reduce | flops 512 | bytes 4096 | tf_op jit(solution)/shard_map/psum | solution.py:18
  101.8 0.6 subtract_reduce_fusion
  103.1 5.9 %convert_bitcast_fusion = bf16[4096,1024]{0,1:T(8,128)(2,1)} fusion(bf16[256,4096]{1,0:T(8,128)(2,1)S(1)} %copy-done, f32[256,1024]{1,0:T(8,128)S(1)} %get-tuple-element.11, f32[256]{0:T(256)S(1)} %bitcast.12, f32[256]{0:T(256)S(1)} %pmax.7, s32[256]{0:T(256)S(1)} %broadcast_subtract_fusion), kind=kOutput, calls=%fused_computation | convolution fusion | flops 2153512960 | bytes 11537408 | tf_op jit(solution)/shard_map/th,tv->hv/dot_general | solution.py:22
  108.9 11.9 %copy.6 = bf16[4096,1024]{1,0:T(8,128)(2,1)} copy(bf16[4096,1024]{0,1:T(8,128)(2,1)} %convert_bitcast_fusion) | data formatting | bytes 16777216
  120.9 7.9 %fusion = f32[256,4096]{1,0:T(8,128)} fusion(bf16[4096,1024]{1,0:T(8,128)(2,1)} %param.4, f32[256,1024]{1,0:T(8,128)S(1)} %get-tuple-element.11, f32[256]{0:T(256)S(1)} %bitcast.13, f32[256]{0:T(256)S(1)} %pmax.7, s32[256]{0:T(256)S(1)} %broadcast_subtract_fusion), kind=kOutput, calls=%fused_computation.9 | convolution fusion | flops 2149318656 | bytes 13634560 | tf_op jit(solution)/shard_map/tv,hv->th/dot_general | solution.py:23
  128.8 78.1 %all-reduce.1 = bf16[256,4096]{1,0:T(8,128)(2,1)} all-reduce(f32[256,4096]{1,0:T(8,128)} %fusion), channel_id=1, replica_groups=mesh['dp'=1,'tp'=32] {'tp'}, use_global_device_ids=true, to_apply=%region_6.7 | all-reduce | flops 1048576 | bytes 6291456 | tf_op jit(solution)/shard_map/psum | solution.py:24
  (4 shorter events, 0.0 us)
Async XLA Ops:
  0.6 1.6 copy-start
  2.2 5.8 %copy-start.1 = (s32[256]{0:T(256)S(1)}, s32[256]{0:T(256)}, u32[]{:S(2)}) copy-start(s32[256]{0:T(256)} %param.5) | copy-start | bytes 3076
where the time goes:
time: 210 us; the launch traced here: 208 us
  blocking collectives  171 us (81%)
  matrix products  19.6 us (9%)
  local copies, waits for them, and re-layouts  13.5 us (6%)
  between operations  2.44 us (1%)
    psum x1, blocking collectives, local(): dX = lax.psum(dXp, 'tp').astype(jnp.bfloat16)  78.1 us
    pmax x1, blocking collectives, local(): M = lax.pmax(m, 'tp')  49.8 us
    psum x1, blocking collectives, local(): st = lax.psum(jnp.stack([s * jnp.exp(m - M), z]), 'tp')  43.5 us
    unnamed x5, local copies, waits for them, and re-layouts  13.5 us
    dot_general x1, matrix products, local(): dXp = jnp.einsum('tv,hv->th', G, W, preferred_element_type=jnp.float32)  7.93 us
    dot_general x1, matrix products, local(): jnp.einsum('th,tv->hv', X, G, preferred_element_type=jnp.float32)  5.86 us
    dot_general x1, matrix products, local(): Z = jnp.dot(X, W, preferred_element_type=jnp.float32)  5.8 us

commit v1 on v0

v1 whole, which is shorter than its diff:
```python
import functools
import math

import jax
import jax.numpy as jnp
from jax import lax
from jax.experimental import pallas as pl
from jax.experimental.pallas import tpu as pltpu
from jax.sharding import PartitionSpec as P

MESH = pl.DeviceIdType.MESH
F32 = jnp.float32
BF16 = jnp.bfloat16
LANES = 128
CORES = 2
NT = (((1,), (1,)), ((), ()))
TN = (((0,), (0,)), ((), ()))


def head_kernel(n_dev, side, X_hbm, W_hbm, lab_ref, L_ref, G_hbm, DX_hbm,
                x_v, w_v, z_v, lab_v, st_v, f_v, msg_v, all_v, g_v,
                own, ds, dr, r1, r2, q_v, t1, t2, dx_v,
                in_sem, w_sem, st_ssem, st_rsem, ssem, rsem, out_sem):
    T, H = x_v.shape
    V = w_v.shape[1]
    R = T // 2
    HC = H // CORES
    U = HC // side
    UH = U // 2
    J = U // side
    RH = R // 2

    me = lax.axis_index('tp')
    c = lax.rem(me, CORES)
    x = lax.rem(me // CORES, side)
    y = me // (CORES * side)
    partner = me + 1 - 2 * c

    def dev(yy, xx):
        return (yy * side + xx) * CORES + c

    def wrap(a):
        return lax.rem(a, side)

    first = (x, y)
    second = (y, x)

    def near1(s, d):
        return dev(y, wrap(x + d)) if s == 0 else dev(wrap(y + d), x)

    def near2(s, d):
        return dev(wrap(y + d), x) if s == 0 else dev(y, wrap(x + d))

    barrier = pltpu.get_barrier_semaphore()

    def greet(i, carry):
        pl.semaphore_signal(barrier, inc=1, device_id={'tp': lax.rem(me + 1 + i, n_dev)}, device_id_type=MESH)
        return carry

    lax.fori_loop(0, n_dev - 1, greet, 0)

    NB = w_sem.shape[0]
    VB = V // NB
    x_in = pltpu.make_async_copy(X_hbm, x_v, in_sem.at[0])
    x_in.start()

    def w_in(i):
        cols = pl.ds(pl.multiple_of(i * VB, VB), VB)
        return pltpu.make_async_copy(W_hbm.at[:, cols], w_v.at[:, cols], w_sem.at[i])

    for i in range(NB):
        w_in(i).start()

    labf = lab_ref[...].astype(F32)
    for b in range(T // LANES):
        row = labf[:, b * LANES:(b + 1) * LANES]
        lab_v[b * LANES:(b + 1) * LANES, :] = jnp.broadcast_to(row, (LANES, LANES)).T

    x_in.wait()

    def logits(i, carry):
        w_in(i).wait()
        cols = pl.ds(pl.multiple_of(i * VB, VB), VB)
        z_v[:, cols] = jnp.dot(x_v[...], w_v[:, cols], preferred_element_type=F32)
        return carry

    lax.fori_loop(0, NB, logits, 0)

    SB = 32
    base = (me * V).astype(F32)
    cols_f = lax.broadcasted_iota(jnp.int32, (SB, V), 1).astype(F32) + base
    lane = lax.broadcasted_iota(jnp.int32, (SB, LANES), 1)

    def stats(i, carry):
        r = pl.ds(pl.multiple_of(i * SB, SB), SB)
        z = z_v[r, :]
        m = jnp.max(z, axis=1, keepdims=True)
        e = jnp.exp(z - m)
        s = jnp.sum(e, axis=1, keepdims=True)
        zt = jnp.sum(jnp.where(cols_f == lab_v[r, 0:1], z, 0.0), axis=1, keepdims=True)
        z_v[r, :] = e
        ln = lane - 4 * (i // (LANES // SB))
        st_v[r, :] = jnp.where(ln == 0, m, jnp.where(ln == 1, s, jnp.where(ln == 2, zt, 0.0)))
        return carry

    lax.fori_loop(0, T // SB, stats, 0)
    msg = st_v[0:LANES, :].T[0:8, :] + st_v[LANES:2 * LANES, :].T[0:8, :]
    msg_v[...] = msg
    all_v[pl.ds(me, 1)] = msg[None]

    pl.semaphore_wait(barrier, n_dev - 1)

    def send_stats(i, carry):
        pltpu.make_async_remote_copy(
            src_ref=msg_v, dst_ref=all_v.at[me], send_sem=st_ssem, recv_sem=st_rsem,
            device_id={'tp': lax.rem(me + 1 + i, n_dev)}, device_id_type=MESH).start()
        return carry

    lax.fori_loop(0, n_dev - 1, send_stats, 0)
    rest = all_v.at[pl.ds(0, n_dev - 1)]
    everybody = pltpu.make_async_remote_copy(
        src_ref=rest, dst_ref=rest, send_sem=st_ssem, recv_sem=st_rsem,
        device_id={'tp': partner}, device_id_type=MESH)
    everybody.wait_recv()

    loss = jnp.zeros((1, 1), F32)
    for b in range(T // LANES):
        m = all_v[:, 4 * b, :]
        s = all_v[:, 4 * b + 1, :]
        zt = jnp.sum(all_v[:, 4 * b + 2, :], axis=0, keepdims=True)
        M = jnp.max(m, axis=0, keepdims=True)
        S = jnp.sum(s * jnp.exp(m - M), axis=0, keepdims=True)
        loss = loss + jnp.sum(M + jnp.log(S) - zt, axis=1, keepdims=True)
        f = jnp.exp(msg_v[4 * b:4 * b + 1, :] - M) / (S * T)
        f_v[b * LANES:(b + 1) * LANES, :] = jnp.broadcast_to(f, (LANES, LANES)).T
    L_ref[...] = loss / T

    def grads(i, carry):
        r = pl.ds(pl.multiple_of(i * SB, SB), SB)
        hit = jnp.where(cols_f == lab_v[r, 0:1], 1.0 / T, 0.0)
        g_v[r, :] = (z_v[r, :] * f_v[r, 0:1] - hit).astype(BF16)
        return carry

    lax.fori_loop(0, T // SB, grads, 0)
    g_out = pltpu.make_async_copy(g_v, G_hbm, out_sem.at[0])
    g_out.start()

    sent = []

    def rcopy(src, dst, to):
        i = len(sent)
        d = pltpu.make_async_remote_copy(src_ref=src, dst_ref=dst, send_sem=ssem.at[i], recv_sem=rsem.at[i],
                                         device_id={'tp': to}, device_id_type=MESH)
        d.start()
        sent.append(d)
        return d

    def unit(k, lo=0, n=U):
        return pl.ds(pl.multiple_of(k * U + lo, LANES), n)

    def part(s, k, core):
        wr = pl.ds(pl.multiple_of(core * HC + k * U, U), U)
        return lax.dot_general(g_v[s * R:(s + 1) * R, :], w_v[wr, :], NT, preferred_element_type=F32)

    pair = {}

    def produce(off):
        for s in (0, 1):
            k = wrap(first[s] + off)
            ds[s, :, unit(k)] = part(s, k, 1 - c)
            pair[s, off] = rcopy(ds.at[s, :, unit(k)], dr.at[s, :, unit(k)], partner)
        for s in (0, 1):
            k = wrap(first[s] + off)
            own[s, :, unit(k)] = part(s, k, c)

    def join(s, off):
        k = wrap(first[s] + off)
        pair[s, off].wait_recv()
        own[s, :, unit(k)] += dr[s, :, unit(k)]

    one = {}
    produce(2)
    produce(1)
    for s in (0, 1):
        join(s, 2)
        k = wrap(first[s] + 2)
        one[s, 0] = rcopy(own.at[s, :, unit(k, 0, UH)], r1.at[s, 0], near1(s, 1))
        one[s, 1] = rcopy(own.at[s, :, unit(k, UH, UH)], r1.at[s, 1], near1(s, side - 1))
    produce(3)
    for s in (0, 1):
        join(s, 1)
        k = wrap(first[s] + 1)
        one[s, 2] = rcopy(own.at[s, :, unit(k, UH, UH)], r2.at[s, 0, :, UH:U], near1(s, 1))
    produce(0)
    for s in (0, 1):
        join(s, 3)
        k = wrap(first[s] + 3)
        one[s, 3] = rcopy(own.at[s, :, unit(k, 0, UH)], r2.at[s, 1, :, 0:UH], near1(s, side - 1))
    for s in (0, 1):
        join(s, 0)
    for s in (0, 1):
        kp = wrap(first[s] + 1)
        km = wrap(first[s] + 3)
        one[s, 0].wait_recv()
        own[s, :, unit(kp, 0, UH)] += r1[s, 0]
        one[s, 4] = rcopy(own.at[s, :, unit(kp, 0, UH)], r2.at[s, 0, :, 0:UH], near1(s, 1))
        one[s, 1].wait_recv()
        own[s, :, unit(km, UH, UH)] += r1[s, 1]
        one[s, 5] = rcopy(own.at[s, :, unit(km, UH, UH)], r2.at[s, 1, :, UH:U], near1(s, side - 1))

    def col2(j):
        return pl.ds(pl.multiple_of(j * J, LANES), J)

    two = {}
    top, bot = slice(0, RH), slice(RH, R)
    for s in (0, 1):
        for i in (2, 3, 4, 5):
            one[s, i].wait_recv()
        q_v[s] = own[s, :, unit(first[s])] + r2[s, 0] + r2[s, 1]
        jo, jp, jm = (wrap(second[s] + d) for d in (2, 1, 3))
        two[s, 0] = rcopy(q_v.at[s, top, col2(jo)], t1.at[s, 0], near2(s, 1))
        two[s, 1] = rcopy(q_v.at[s, bot, col2(jo)], t1.at[s, 1], near2(s, side - 1))
        two[s, 2] = rcopy(q_v.at[s, bot, col2(jp)], t2.at[s, 0, bot], near2(s, 1))
        two[s, 3] = rcopy(q_v.at[s, top, col2(jm)], t2.at[s, 1, top], near2(s, side - 1))
    for s in (0, 1):
        jp, jm = (wrap(second[s] + d) for d in (1, 3))
        two[s, 0].wait_recv()
        q_v[s, top, col2(jp)] += t1[s, 0]
        two[s, 4] = rcopy(q_v.at[s, top, col2(jp)], t2.at[s, 0, top], near2(s, 1))
        two[s, 1].wait_recv()
        q_v[s, bot, col2(jm)] += t1[s, 1]
        two[s, 5] = rcopy(q_v.at[s, bot, col2(jm)], t2.at[s, 1, bot], near2(s, side - 1))

    def at2(s, j, half):
        rows = slice(s * R + half * RH, s * R + (half + 1) * RH)
        return dx_v.at[rows, pl.ds(pl.multiple_of(c * HC + first[s] * U + j * J, LANES), J)]

    def at1(s, k, half):
        return dx_v.at[s * R:(s + 1) * R, pl.ds(pl.multiple_of(c * HC + k * U + half * UH, LANES), UH)]

    def block(s, k):
        return pl.ds(pl.multiple_of(c * HC + k * U, LANES), U)

    three = {}
    for s in (0, 1):
        j = second[s]
        for i in (2, 3, 4, 5):
            two[s, i].wait_recv()
        total = q_v[s, :, col2(j)] + t2[s, 0] + t2[s, 1]
        dx_v[s * R:(s + 1) * R, pl.ds(pl.multiple_of(c * HC + first[s] * U + j * J, LANES), J)] = total.astype(BF16)
        three[s, 0] = rcopy(at2(s, j, 0), at2(s, j, 0), near2(s, 1))
        three[s, 1] = rcopy(at2(s, j, 1), at2(s, j, 1), near2(s, side - 1))
        three[s, 2] = rcopy(at2(s, j, 1), at2(s, j, 1), near2(s, 1))
        three[s, 3] = rcopy(at2(s, j, 0), at2(s, j, 0), near2(s, side - 1))
    for s in (0, 1):
        jp, jm = (wrap(second[s] + d) for d in (1, 3))
        three[s, 0].wait_recv()
        three[s, 4] = rcopy(at2(s, jm, 0), at2(s, jm, 0), near2(s, 1))
        three[s, 1].wait_recv()
        three[s, 5] = rcopy(at2(s, jp, 1), at2(s, jp, 1), near2(s, side - 1))

    outs = []

    def put(s, cols):
        d = pltpu.make_async_copy(dx_v.at[s * R:(s + 1) * R, cols], DX_hbm.at[s * R:(s + 1) * R, cols],
                                  out_sem.at[1 + len(outs)])
        d.start()
        outs.append(d)

    four = {}
    pairs = []

    def share(s, k):
        ref = dx_v.at[s * R:(s + 1) * R, block(s, k)]
        pairs.append((s, k, rcopy(ref, ref, partner)))
        put(s, block(s, k))

    for s in (0, 1):
        for i in (2, 3, 4, 5):
            three[s, i].wait_recv()
        k = first[s]
        four[s, 0] = rcopy(at1(s, k, 0), at1(s, k, 0), near1(s, 1))
        four[s, 1] = rcopy(at1(s, k, 1), at1(s, k, 1), near1(s, side - 1))
        four[s, 2] = rcopy(at1(s, k, 1), at1(s, k, 1), near1(s, 1))
        four[s, 3] = rcopy(at1(s, k, 0), at1(s, k, 0), near1(s, side - 1))
        share(s, k)
    for s in (0, 1):
        kp, km = (wrap(first[s] + d) for d in (1, 3))
        four[s, 0].wait_recv()
        four[s, 4] = rcopy(at1(s, km, 0), at1(s, km, 0), near1(s, 1))
        four[s, 1].wait_recv()
        four[s, 5] = rcopy(at1(s, kp, 1), at1(s, kp, 1), near1(s, side - 1))
    for s in (0, 1):
        four[s, 2].wait_recv()
        share(s, wrap(first[s] + 3))
        four[s, 3].wait_recv()
        share(s, wrap(first[s] + 1))
    for s in (0, 1):
        four[s, 4].wait_recv()
        four[s, 5].wait_recv()
        share(s, wrap(first[s] + 2))
    for s, k, d in pairs:
        d.wait_recv()
        put(s, pl.ds(pl.multiple_of((1 - c) * HC + k * U, LANES), U))

    everybody.wait_send()
    for d in sent:
        d.wait_send()
    g_out.wait()
    for d in outs:
        d.wait()


N_COPIES = 8 + 4 * 12 + 8
N_OUTS = 1 + 16


def dw_kernel(x_ref, g_ref, o_ref):
    o_ref[...] = lax.dot_general(x_ref[...], g_ref[...], TN, preferred_element_type=F32).astype(BF16)


def solution(mesh):
    n_dev = mesh.shape['tp']
    side = math.isqrt(n_dev // CORES)

    def local(X, W, labels):
        T, H = X.shape
        V = W.shape[1]
        R, HC = T // 2, H // CORES
        U = HC // side
        J = U // side
        any_ = pl.BlockSpec(memory_space=pl.ANY)
        vmem = pl.BlockSpec(memory_space=pltpu.VMEM)
        L, G, dX = pl.pallas_call(
            functools.partial(head_kernel, n_dev, side),
            name='head',
            out_shape=(jax.ShapeDtypeStruct((1, 1), F32), jax.ShapeDtypeStruct((T, V), BF16),
                       jax.ShapeDtypeStruct((T, H), BF16)),
            in_specs=[any_, any_, vmem],
            out_specs=(vmem, any_, any_),
            scratch_shapes=[
                pltpu.VMEM((T, H), BF16), pltpu.VMEM((H, V), BF16), pltpu.VMEM((T, V), F32),
                pltpu.VMEM((T, LANES), F32), pltpu.VMEM((T, LANES), F32), pltpu.VMEM((T, LANES), F32),
                pltpu.VMEM((8, LANES), F32), pltpu.VMEM((n_dev, 8, LANES), F32), pltpu.VMEM((T, V), BF16),
                pltpu.VMEM((2, R, HC), F32), pltpu.VMEM((2, R, HC), F32), pltpu.VMEM((2, R, HC), F32),
                pltpu.VMEM((2, 2, R, U // 2), F32), pltpu.VMEM((2, 2, R, U), F32), pltpu.VMEM((2, R, U), F32),
                pltpu.VMEM((2, 2, R // 2, J), F32), pltpu.VMEM((2, 2, R, J), F32), pltpu.VMEM((T, H), BF16),
                pltpu.SemaphoreType.DMA((1,)), pltpu.SemaphoreType.DMA((4,)),
                pltpu.SemaphoreType.DMA, pltpu.SemaphoreType.DMA,
                pltpu.SemaphoreType.DMA((N_COPIES,)), pltpu.SemaphoreType.DMA((N_COPIES,)),
                pltpu.SemaphoreType.DMA((N_OUTS,)),
            ],
            compiler_params=pltpu.CompilerParams(collective_id=0, has_side_effects=True,
                                                 vmem_limit_bytes=48 * 1024 * 1024),
        )(X, W, labels.reshape(1, T))

        HB = H // 8
        dW = pl.pallas_call(
            dw_kernel,
            name='dw',
            out_shape=jax.ShapeDtypeStruct((H, V), BF16),
            grid=(H // HB,),
            in_specs=[pl.BlockSpec((T, HB), lambda i: (0, i)), pl.BlockSpec((T, V), lambda i: (0, 0))],
            out_specs=pl.BlockSpec((HB, V), lambda i: (i, 0)),
            compiler_params=pltpu.CompilerParams(dimension_semantics=('arbitrary',)),
        )(X, G)
        return L.reshape(1), dW, dX

    return jax.shard_map(local, mesh=mesh,
                         in_specs=(P('dp', None), P(None, 'tp'), P('dp')),
                         out_specs=(P('dp'), P('dp', 'tp'), P('dp', None)),
                         check_vma=False)
```

time: 210 us -> 73.7 us (0.35)
  blocking collectives: 171 us -> 0 us
  Pallas kernels: 0 us -> 66.6 us
  matrix products: 19.6 us -> 0 us
  local copies, waits for them, and re-layouts: 13.5 us -> 4.37 us
    psum x2 -> x0, blocking collectives: 122 us -> none  [the longest x1 78.1 us: local(): dX = lax.psum(dXp, 'tp').astype(jnp.bfloat16)]
    pallas_call x0 -> x2, Pallas kernels: none -> 66.6 us  [the longest x1 58.2 us: local(): pl.pallas_call(functools.partial(head_kernel, n_dev, side), name='head',...]
    pmax x1 -> x0, blocking collectives: 49.8 us -> none  [local(): M = lax.pmax(m, 'tp')]
    dot_general x3 -> x0, matrix products: 19.6 us -> none  [the longest x1 7.93 us: local(): dXp = jnp.einsum('tv,hv->th', G, W, preferred_element_type=jnp.float32)]
    unnamed x5 -> x7, local copies, waits for them, and re-layouts: 13.5 us -> 4.37 us
where the time goes in v1:
time: 73.7 us; the launch traced here: 73.4 us
  Pallas kernels  66.6 us (90%)
  local copies, waits for them, and re-layouts  4.37 us (6%)
  between operations  2.4 us (3%)
    pallas_call x1, Pallas kernels, local(): pl.pallas_call(functools.partial(head_kernel, n_dev, side), name='head',...  58.2 us
    pallas_call x1, Pallas kernels, local(): pl.pallas_call(dw_kernel, name='dw', out_shape=jax.ShapeDtypeStruct((H, V...  8.4 us
    unnamed x7, local copies, waits for them, and re-layouts  4.37 us

profile of v1, /device:TPU:97, one launch (start us, length us, event | category | flops | bytes accessed | tf_op | source)
XLA Modules:
  0.0 73.4 jit_solution(11090409281047370282)
XLA Ops:
  0.6 0.0 copy-start
  0.6 1.6 %copy-done = bf16[256,4096]{1,0:T(8,128)(2,1)S(1)} copy-done((bf16[256,4096]{1,0:T(8,128)(2,1)S(1)}, bf16[256,4096]{1,0:T(8,128)(2,1)}, u32[]{:S(2)}) %copy-start) | copy-done | bytes 2097176
  2.2 0.0 copy-start.2
  2.2 0.7 copy-done.2
  2.9 58.2 %head.1 = (f32[1,1]{1,0:T(1,128)}, bf16[256,1024]{1,0:T(8,128)(2,1)S(1)}, bf16[256,4096]{1,0:T(8,128)(2,1)S(1)}) custom-call(bf16[256,4096]{1,0:T(8,128)(2,1)S(1)} %copy-done, bf16[4096,1024]{1,0:T(8,128)(2,1)} %W_hbm.1, s32[1,256]{1,0:T(1,128)S(1)} %bitcast.2), custom_call_target="tpu_custom_call" | custom-call | tf_op jit(solution)/shard_map/head/pallas_call | solution.py:334
  61.1 0.0 copy-start.1
  61.1 0.8 %copy-done.1 = bf16[256,1024]{1,0:T(8,128)(2,1)} copy-done((bf16[256,1024]{1,0:T(8,128)(2,1)}, bf16[256,1024]{1,0:T(8,128)(2,1)S(1)}, u32[]{:S(2)}) %copy-start.1) | copy-done | bytes 524312
  61.9 8.4 %dw.1 = bf16[4096,1024]{1,0:T(8,128)(2,1)} custom-call(bf16[256,4096]{1,0:T(8,128)(2,1)} %x_ref.1, bf16[256,1024]{1,0:T(8,128)(2,1)} %copy-done.1), custom_call_target="tpu_custom_call" | custom-call | tf_op jit(solution)/shard_map/dw/pallas_call | solution.py:358
  70.9 1.3 %copy.9 = bf16[256,4096]{1,0:T(8,128)(2,1)} copy(bf16[256,4096]{1,0:T(8,128)(2,1)S(1)} %get-tuple-element.14) | data formatting | bytes 4194304
Async XLA Ops:
  0.6 1.6 %copy-start = (bf16[256,4096]{1,0:T(8,128)(2,1)S(1)}, bf16[256,4096]{1,0:T(8,128)(2,1)}, u32[]{:S(2)}) copy-start(bf16[256,4096]{1,0:T(8,128)(2,1)} %x_ref.1) | copy-start | bytes 6291460
  2.2 0.7 copy-start.2
  61.1 0.8 %copy-start.1 = (bf16[256,1024]{1,0:T(8,128)(2,1)}, bf16[256,1024]{1,0:T(8,128)(2,1)S(1)}, u32[]{:S(2)}) copy-start(bf16[256,1024]{1,0:T(8,128)(2,1)S(1)} %get-tuple-element.7.g_ref) | copy-start | bytes 1572868

commit v2 on v1

--- a/solution.py
+++ b/solution.py
@@ -17,10 +17,10 @@
 TN = (((0,), (0,)), ((), ()))
 
 
-def head_kernel(n_dev, side, X_hbm, W_hbm, lab_ref, L_ref, G_hbm, DX_hbm,
-                x_v, w_v, z_v, lab_v, st_v, f_v, msg_v, all_v, g_v,
-                own, ds, dr, r1, r2, q_v, t1, t2, dx_v,
-                in_sem, w_sem, st_ssem, st_rsem, ssem, rsem, out_sem):
+def head_kernel(n_dev, side, X_hbm, W_hbm, lab_hbm, L_ref, dw_v, dx_v,
+                x_v, w_v, xt_v, z_v, labr_v, lab_v, st_v, f_v, msg_v, all_v, g_v,
+                own, ds, dr, r1, r2, q_v, t1, t2,
+                in_sem, w_sem, st_ssem, st_rsem, ssem, rsem):
     T, H = x_v.shape
     V = w_v.shape[1]
     R = T // 2
@@ -63,6 +63,8 @@
     VB = V // NB
     x_in = pltpu.make_async_copy(X_hbm, x_v, in_sem.at[0])
     x_in.start()
+    lab_in = pltpu.make_async_copy(lab_hbm, labr_v, in_sem.at[1])
+    lab_in.start()
 
     def w_in(i):
         cols = pl.ds(pl.multiple_of(i * VB, VB), VB)
@@ -71,7 +73,8 @@
     for i in range(NB):
         w_in(i).start()
 
-    labf = lab_ref[...].astype(F32)
+    lab_in.wait()
+    labf = labr_v[...].astype(F32)
     for b in range(T // LANES):
         row = labf[:, b * LANES:(b + 1) * LANES]
         lab_v[b * LANES:(b + 1) * LANES, :] = jnp.broadcast_to(row, (LANES, LANES)).T
@@ -117,6 +120,15 @@
         return carry
 
     lax.fori_loop(0, n_dev - 1, send_stats, 0)
+
+    XB = 256
+
+    def flip(i, carry):
+        r = pl.ds(pl.multiple_of(i * XB, XB), XB)
+        xt_v[r, :] = x_v[:, r].T
+        return carry
+
+    lax.fori_loop(0, H // XB, flip, 0)
     rest = all_v.at[pl.ds(0, n_dev - 1)]
     everybody = pltpu.make_async_remote_copy(
         src_ref=rest, dst_ref=rest, send_sem=st_ssem, recv_sem=st_rsem,
@@ -142,8 +154,6 @@
         return carry
 
     lax.fori_loop(0, T // SB, grads, 0)
-    g_out = pltpu.make_async_copy(g_v, G_hbm, out_sem.at[0])
-    g_out.start()
 
     sent = []
 
@@ -161,6 +171,16 @@
     def part(s, k, core):
         wr = pl.ds(pl.multiple_of(core * HC + k * U, U), U)
         return lax.dot_general(g_v[s * R:(s + 1) * R, :], w_v[wr, :], NT, preferred_element_type=F32)
+
+    DB = H // 8
+
+    def dw_rows(lo, hi):
+        def step(i, carry):
+            r = pl.ds(pl.multiple_of(i * DB, DB), DB)
+            dw_v[r, :] = jnp.dot(xt_v[r, :], g_v[...], preferred_element_type=F32).astype(BF16)
+            return carry
+
+        lax.fori_loop(lo, hi, step, 0)
 
     pair = {}
 
@@ -198,6 +218,7 @@
         one[s, 3] = rcopy(own.at[s, :, unit(k, 0, UH)], r2.at[s, 1, :, 0:UH], near1(s, side - 1))
     for s in (0, 1):
         join(s, 0)
+    dw_rows(0, 4)
     for s in (0, 1):
         kp = wrap(first[s] + 1)
         km = wrap(first[s] + 3)
@@ -207,6 +228,8 @@
         one[s, 1].wait_recv()
         own[s, :, unit(km, UH, UH)] += r1[s, 1]
         one[s, 5] = rcopy(own.at[s, :, unit(km, UH, UH)], r2.at[s, 1, :, UH:U], near1(s, side - 1))
+
+    dw_rows(4, 8)
 
     def col2(j):
         return pl.ds(pl.multiple_of(j * J, LANES), J)
@@ -259,21 +282,12 @@
         three[s, 1].wait_recv()
         three[s, 5] = rcopy(at2(s, jp, 1), at2(s, jp, 1), near2(s, side - 1))
 
-    outs = []
-
-    def put(s, cols):
-        d = pltpu.make_async_copy(dx_v.at[s * R:(s + 1) * R, cols], DX_hbm.at[s * R:(s + 1) * R, cols],
-                                  out_sem.at[1 + len(outs)])
-        d.start()
-        outs.append(d)
-
     four = {}
     pairs = []
 
     def share(s, k):
         ref = dx_v.at[s * R:(s + 1) * R, block(s, k)]
-        pairs.append((s, k, rcopy(ref, ref, partner)))
-        put(s, block(s, k))
+        pairs.append(rcopy(ref, ref, partner))
 
     for s in (0, 1):
         for i in (2, 3, 4, 5):
@@ -299,24 +313,28 @@
         four[s, 4].wait_recv()
         four[s, 5].wait_recv()
         share(s, wrap(first[s] + 2))
-    for s, k, d in pairs:
+    for d in pairs:
         d.wait_recv()
-        put(s, pl.ds(pl.multiple_of((1 - c) * HC + k * U, LANES), U))
 
     everybody.wait_send()
     for d in sent:
         d.wait_send()
-    g_out.wait()
-    for d in outs:
+
+
+N_COPIES = 8 + 4 * 12 + 8
+N_PUT = 8
+
+
+def put_kernel(l_ref, dw_ref, dx_ref, l_hbm, dw_hbm, dx_hbm, sem):
+    n = dw_ref.shape[0] // N_PUT
+    copies = [pltpu.make_async_copy(dw_ref.at[i * n:(i + 1) * n], dw_hbm.at[i * n:(i + 1) * n], sem.at[i])
+              for i in range(N_PUT)]
+    copies.append(pltpu.make_async_copy(dx_ref, dx_hbm, sem.at[N_PUT]))
+    copies.append(pltpu.make_async_copy(l_ref, l_hbm, sem.at[N_PUT + 1]))
+    for d in copies:
+        d.start()
+    for d in copies:
         d.wait()
-
-
-N_COPIES = 8 + 4 * 12 + 8
-N_OUTS = 1 + 16
-
-
-def dw_kernel(x_ref, g_ref, o_ref):
-    o_ref[...] = lax.dot_general(x_ref[...], g_ref[...], TN, preferred_element_type=F32).astype(BF16)
 
 
 def solution(mesh):
@@ -329,41 +347,40 @@
         R, HC = T // 2, H // CORES
         U = HC // side
         J = U // side
-        any_ = pl.BlockSpec(memory_space=pl.ANY)
         vmem = pl.BlockSpec(memory_space=pltpu.VMEM)
-        L, G, dX = pl.pallas_call(
+        hbm = pl.BlockSpec(memory_space=pltpu.HBM)
+        L, dW, dX = pl.pallas_call(
             functools.partial(head_kernel, n_dev, side),
             name='head',
-            out_shape=(jax.ShapeDtypeStruct((1, 1), F32), jax.ShapeDtypeStruct((T, V), BF16),
-                       jax.ShapeDtypeStruct((T, H), BF16)),
-            in_specs=[any_, any_, vmem],
-            out_specs=(vmem, any_, any_),
+            out_shape=(pltpu.VMEM((1, 1), F32), pltpu.VMEM((H, V), BF16), pltpu.VMEM((T, H), BF16)),
+            in_specs=[hbm, hbm, hbm],
+            out_specs=(vmem, vmem, vmem),
             scratch_shapes=[
-                pltpu.VMEM((T, H), BF16), pltpu.VMEM((H, V), BF16), pltpu.VMEM((T, V), F32),
+                pltpu.VMEM((T, H), BF16), pltpu.VMEM((H, V), BF16), pltpu.VMEM((H, T), BF16), pltpu.VMEM((T, V), F32),
+                pltpu.VMEM((1, T), jnp.int32),
                 pltpu.VMEM((T, LANES), F32), pltpu.VMEM((T, LANES), F32), pltpu.VMEM((T, LANES), F32),
                 pltpu.VMEM((8, LANES), F32), pltpu.VMEM((n_dev, 8, LANES), F32), pltpu.VMEM((T, V), BF16),
                 pltpu.VMEM((2, R, HC), F32), pltpu.VMEM((2, R, HC), F32), pltpu.VMEM((2, R, HC), F32),
                 pltpu.VMEM((2, 2, R, U // 2), F32), pltpu.VMEM((2, 2, R, U), F32), pltpu.VMEM((2, R, U), F32),
-                pltpu.VMEM((2, 2, R // 2, J), F32), pltpu.VMEM((2, 2, R, J), F32), pltpu.VMEM((T, H), BF16),
-                pltpu.SemaphoreType.DMA((1,)), pltpu.SemaphoreType.DMA((4,)),
+                pltpu.VMEM((2, 2, R // 2, J), F32), pltpu.VMEM((2, 2, R, J), F32),
+                pltpu.SemaphoreType.DMA((2,)), pltpu.SemaphoreType.DMA((4,)),
                 pltpu.SemaphoreType.DMA, pltpu.SemaphoreType.DMA,
                 pltpu.SemaphoreType.DMA((N_COPIES,)), pltpu.SemaphoreType.DMA((N_COPIES,)),
-                pltpu.SemaphoreType.DMA((N_OUTS,)),
             ],
             compiler_params=pltpu.CompilerParams(collective_id=0, has_side_effects=True,
-                                                 vmem_limit_bytes=48 * 1024 * 1024),
-        )(X, W, labels.reshape(1, T))
-
-        HB = H // 8
-        dW = pl.pallas_call(
-            dw_kernel,
-            name='dw',
-            out_shape=jax.ShapeDtypeStruct((H, V), BF16),
-            grid=(H // HB,),
-            in_specs=[pl.BlockSpec((T, HB), lambda i: (0, i)), pl.BlockSpec((T, V), lambda i: (0, 0))],
-            out_specs=pl.BlockSpec((HB, V), lambda i: (i, 0)),
-            compiler_params=pltpu.CompilerParams(dimension_semantics=('arbitrary',)),
-        )(X, G)
+                                                 vmem_limit_bytes=40 * 1024 * 1024),
+        )(*(pltpu.with_memory_space_constraint(a, pltpu.HBM) for a in (X, W, labels.reshape(1, T))))
+
+        L, dW, dX = pl.pallas_call(
+            put_kernel,
+            name='put',
+            out_shape=(jax.ShapeDtypeStruct((1, 1), F32), jax.ShapeDtypeStruct((H, V), BF16),
+                       jax.ShapeDtypeStruct((T, H), BF16)),
+            in_specs=[vmem, vmem, vmem],
+            out_specs=(hbm, hbm, hbm),
+            scratch_shapes=[pltpu.SemaphoreType.DMA((N_PUT + 2,))],
+            compiler_params=pltpu.CompilerParams(vmem_limit_bytes=1024 * 1024),
+        )(*(pltpu.with_memory_space_constraint(a, pltpu.VMEM) for a in (L, dW, dX)))
         return L.reshape(1), dW, dX
 
     return jax.shard_map(local, mesh=mesh,

time: 73.7 us -> 65.3 us (0.89)
  local copies, waits for them, and re-layouts: 4.37 us -> 0 us
  Pallas kernels: 66.6 us -> 64.5 us
  between operations: 2.4 us -> 0.64 us
    unnamed x7 -> x0, local copies, waits for them, and re-layouts: 4.37 us -> none
    pallas_call x1, Pallas kernels: 8.4 us -> 4.68 us  [local(): pl.pallas_call(put_kernel, name='put', out_shape=(jax.ShapeDtypeStruct((1...]
    pallas_call x1, Pallas kernels: 58.2 us -> 59.8 us  [local(): pl.pallas_call(functools.partial(head_kernel, n_dev, side), name='head',...]
where the time goes in v2:
time: 65.3 us; the launch traced here: 65.2 us
  Pallas kernels  64.5 us (99%)
    pallas_call x1, Pallas kernels, local(): pl.pallas_call(functools.partial(head_kernel, n_dev, side), name='head',...  59.8 us
    pallas_call x1, Pallas kernels, local(): pl.pallas_call(put_kernel, name='put', out_shape=(jax.ShapeDtypeStruct((1...  4.68 us

profile of v2, /device:TPU:97, one launch (start us, length us, event | category | flops | bytes accessed | tf_op | source)
XLA Modules:
  0.0 65.2 jit_solution(13880306210467961190)
XLA Ops:
  0.6 59.8 %head.1 = (f32[1,1]{1,0:T(1,128)}, bf16[4096,1024]{1,0:T(8,128)(2,1)S(1)}, bf16[256,4096]{1,0:T(8,128)(2,1)S(1)}) custom-call(bf16[256,4096]{1,0:T(8,128)(2,1)} %X_hbm.1, bf16[4096,1024]{1,0:T(8,128)(2,1)} %W_hbm.1, s32[1,256]{1,0:T(1,128)} %bitcast.2), custom_call_target="tpu_custom_call" | custom-call | tf_op jit(solution)/shard_map/head/pallas_call | solution.py:352
  60.5 4.7 %put.1 = (f32[1,1]{1,0:T(1,128)}, bf16[4096,1024]{1,0:T(8,128)(2,1)}, bf16[256,4096]{1,0:T(8,128)(2,1)}) custom-call(f32[1,1]{1,0:T(1,128)} %get-tuple-element.9.l_ref, bf16[4096,1024]{1,0:T(8,128)(2,1)S(1)} %get-tuple-element.10.dw_ref, bf16[256,4096]{1,0:T(8,128)(2,1)S(1)} %get-tuple-element.11.dx_ref), custom_call_target="tpu_custom_call" | custom-call | tf_op jit(solution)/shard_map/put/pallas_call | solution.py:374
